TPU v7x, 256 devices: a whole 4x4x8 slice. The times are simulated.
256 devices in a mesh: horiz: 32 (over x, y, core), lev: 8 (over z).
Axes of the slice: x: 4, y: 4, z: 8, core: 2. Of those that a mesh axis runs over, the one named last changes fastest.
Arguments:
- source_state: bfloat16 [5, 136, 131072], P(None, 'lev', 'horiz'), may hold values from -6 to 6
- intersection: int32 [160], P('horiz'), may hold values from 0 to 31, as said below
- index_map: int32 [160, 512], P('horiz'), may hold values from 0 to 4095
- blocks: bfloat16 [160, 512, 2048], P('horiz'), may hold values from -0.125 to 0.125
- bracket: int32 [127, 65536], P(None, ('horiz', 'lev')), may hold values from 0 to 134
- fraction: float32 [127, 65536], P(None, ('horiz', 'lev')), may hold values from 0 to 1
Outputs:
- target_state: bfloat16 [5, 127, 65536], P(None, None, ('horiz', 'lev'))
Inputs may be any that keep to these rules, and one draw needn't show every extreme that they name: For every target group g, intersection[g * 5] to intersection[g * 5 + 4] are the groups g - 2 to g + 2 modulo 32, each once, in some order.
All inputs are finite; a program needn't handle non-finite values.
Results may differ from a plain program's by a relative error of at most 0.0049.
Values may be sent and summed in bfloat16 or wider, within the bound.
A program may use at most 64 MiB of HBM per device.

v0:
```python
import jax
import jax.numpy as jnp
from jax import lax
from jax.sharding import PartitionSpec as P


def shifted(block, axis, distance):
    devices = range(lax.axis_size(axis))
    route = [((i - distance) % len(devices), i) for i in devices]
    return lax.ppermute(block, axis, route)


def select_cells(tile, wanted):
    cell_ids = jnp.arange(tile.shape[1], dtype=jnp.int32)[:, None]
    picker = (cell_ids == wanted[None, :]).astype(jnp.bfloat16)
    return jnp.dot(tile, picker, preferred_element_type=jnp.float32).astype(jnp.bfloat16)


def local(source_state, intersection, index_map, blocks, bracket, fraction):
    fields, level_slab, tile_cells = source_state.shape
    stacked = source_state.reshape(fields * level_slab, tile_cells)
    groups = lax.axis_size("horiz")
    block_count = intersection.shape[0]
    depth = (block_count - 1) // 2
    own_group = lax.axis_index("horiz")
    position = (intersection - own_group + depth) % groups
    collected = []
    for offset in range(-depth, depth + 1):
        wanted_group = (own_group + offset) % groups
        matched = intersection == wanted_group
        request = jnp.sum(jnp.where(matched[:, None], index_map, 0), axis=0)
        if offset == 0:
            collected.append(select_cells(stacked, request))
        else:
            incoming = shifted(request, "horiz", offset)
            outgoing = select_cells(stacked, incoming)
            collected.append(shifted(outgoing, "horiz", -offset))
    by_offset = jnp.stack(collected)
    pieces = [
        lax.dynamic_index_in_dim(by_offset, position[block_slot], 0, keepdims=False)
        for block_slot in range(block_count)
    ]
    chosen = jnp.concatenate(pieces, axis=1)
    weights_flat = blocks.reshape(-1, blocks.shape[2])
    horizontal = jnp.dot(chosen, weights_flat, preferred_element_type=jnp.float32).astype(
        jnp.bfloat16
    )
    horizontal = horizontal.reshape(fields, level_slab, blocks.shape[2])
    level_total = level_slab * lax.axis_size("lev")
    level_ids = jnp.arange(level_total, dtype=jnp.int32)[None, :, None]
    lower_hit = level_ids == bracket[:, None, :]
    upper_hit = level_ids == bracket[:, None, :] + 1
    upper_share = fraction[:, None, :]
    interp = jnp.where(lower_hit, 1.0 - upper_share, 0.0) + jnp.where(upper_hit, upper_share, 0.0)
    widened = lax.all_to_all(horizontal, "lev", split_axis=2, concat_axis=1, tiled=True).astype(
        jnp.float32
    )
    mixed = jnp.einsum("jlc,flc->fjc", interp, widened, precision=lax.Precision.HIGHEST)
    return mixed.astype(jnp.bfloat16)


def solution(mesh):
    in_specs = (
        P(None, "lev", "horiz"),
        P("horiz"),
        P("horiz", None),
        P("horiz", None, None),
        P(None, ("horiz", "lev")),
        P(None, ("horiz", "lev")),
    )
    out_specs = P(None, None, ("horiz", "lev"))
    return jax.shard_map(local, mesh=mesh, in_specs=in_specs, out_specs=out_specs, check_vma=False)
```

profile of v0, /device:TPU:30, one launch (start us, length us, event | category | flops | bytes accessed | tf_op | source)
XLA Modules:
  0.0 92.4 jit_solution(9998000681186927857)
XLA Ops:
  0.7 0.8 select_reduce_fusion
  2.5 4.6 %collective-permute-start.6 = (s32[512]{0:T(512)S(1)}, s32[512]{0:T(512)S(1)}, u32[]{:S(2)}, u32[]{:S(2)}) collective-permute-start(s32[512]{0:T(512)S(1)} %get-tuple-element.5), channel_id=1, source_target_pairs={{240,0},{248,8},{0,16},{8,24},{16,32},{24,40},{32,48},{40,56},{48,... | collective-permute-start | bytes 6152 | tf_op jit(solution)/shard_map/ppermute | solution.py:10
  7.1 0.7 and_select_fusion
  7.8 0.7 fusion.38
  14.9 1.4 %reshape.25 = bf16[85,4096]{1,0:T(8,128)(2,1)S(1)} reshape(bf16[5,17,4096]{2,1,0:T(8,128)(2,1)} %param.6) | data formatting | bytes 1392640 | tf_op jit(solution)/shard_map/reshape | solution.py:21
  19.6 1.5 %fusion.31 = bf16[85,512]{1,0:T(8,128)(2,1)S(1)} fusion(bf16[85,4096]{1,0:T(8,128)(2,1)S(1)} %reshape.25, s32[512]{0:T(512)S(1)} %collective-permute-done.2), kind=kOutput, calls=%fused_computation.35 | convolution fusion | flops 358656512 | bytes 785408 | tf_op jit(solution)/shard_map/dot_general | solution.py:16
  21.1 1.1 %collective-permute-start.3 = (bf16[85,512]{1,0:T(8,128)(2,1)S(1)}, bf16[85,512]{1,0:T(8,128)(2,1)S(1)}, u32[]{:S(2)}, u32[]{:S(2)}) collective-permute-start(bf16[85,512]{1,0:T(8,128)(2,1)S(1)} %fusion.31), channel_id=1, source_target_pairs={{248,0},{0,8},{8,16},{16,24},{24,32},{32,40},{40,48},{48,56},{56,6... | collective-permute-start | bytes 261128 | tf_op jit(solution)/shard_map/ppermute | solution.py:10
  22.2 1.5 %fusion.30 = bf16[85,512]{1,0:T(8,128)(2,1)S(1)} fusion(bf16[85,4096]{1,0:T(8,128)(2,1)S(1)} %reshape.25, s32[512]{0:T(512)S(1)} %collective-permute-done), kind=kOutput, calls=%fused_computation.34 | convolution fusion | flops 358656512 | bytes 785408 | tf_op jit(solution)/shard_map/dot_general | solution.py:16
  24.1 1.5 %fusion.34 = bf16[85,512]{1,0:T(8,128)(2,1)S(1)} fusion(bf16[85,4096]{1,0:T(8,128)(2,1)S(1)} %reshape.25, s32[512]{0:T(512)S(1)} %collective-permute-done.4), kind=kOutput, calls=%fused_computation.38 | convolution fusion | flops 358656512 | bytes 785408 | tf_op jit(solution)/shard_map/dot_general | solution.py:16
  25.5 1.4 %collective-permute-start.5 = (bf16[85,512]{1,0:T(8,128)(2,1)S(1)}, bf16[85,512]{1,0:T(8,128)(2,1)S(1)}, u32[]{:S(2)}, u32[]{:S(2)}) collective-permute-start(bf16[85,512]{1,0:T(8,128)(2,1)S(1)} %fusion.34), channel_id=1, source_target_pairs={{8,0},{16,8},{24,16},{32,24},{40,32},{48,40},{56,48},{64,56},{72,6... | collective-permute-start | bytes 261128 | tf_op jit(solution)/shard_map/ppermute | solution.py:10
  27.0 1.5 %fusion.35 = bf16[85,512]{1,0:T(8,128)(2,1)S(1)} fusion(bf16[85,4096]{1,0:T(8,128)(2,1)S(1)} %reshape.25, s32[512]{0:T(512)S(1)} %collective-permute-done.6), kind=kOutput, calls=%fused_computation.39 | convolution fusion | flops 358656512 | bytes 785408 | tf_op jit(solution)/shard_map/dot_general | solution.py:16
  28.5 1.0 %collective-permute-start.7 = (bf16[85,512]{1,0:T(8,128)(2,1)S(1)}, bf16[85,512]{1,0:T(8,128)(2,1)S(1)}, u32[]{:S(2)}, u32[]{:S(2)}) collective-permute-start(bf16[85,512]{1,0:T(8,128)(2,1)S(1)} %fusion.35), channel_id=1, source_target_pairs={{16,0},{24,8},{32,16},{40,24},{48,32},{56,40},{64,48},{72,56},{80,... | collective-permute-start | bytes 261128 | tf_op jit(solution)/shard_map/ppermute | solution.py:10
  29.5 1.5 %fusion.33 = bf16[5,85,512]{2,1,0:T(8,128)(2,1)S(1)} fusion(bf16[5,85,512]{2,1,0:T(8,128)(2,1)S(1)} %bitcast_dynamic-update-slice_fusion.7, bf16[85,4096]{1,0:T(8,128)(2,1)S(1)} %reshape.25, s32[512]{0:T(512)S(1)} %get-tuple-element.6), kind=kOutput, calls=%fused_computation.37 | convolution fusion | flops 358656512 | bytes 813056 | tf_op jit(solution)/shard_map/dot_general | solution.py:16
  31.0 5.5 %collective-permute-done.7 = bf16[85,512]{1,0:T(8,128)(2,1)S(1)} collective-permute-done((bf16[85,512]{1,0:T(8,128)(2,1)S(1)}, bf16[85,512]{1,0:T(8,128)(2,1)S(1)}, u32[]{:S(2)}, u32[]{:S(2)}) %collective-permute-start.7) | collective-permute-done | bytes 87072 | tf_op jit(solution)/shard_map/ppermute | solution.py:10
  36.7 1.9 %convolution_convert_fusion = bf16[85,2048]{1,0:T(8,128)(2,1)S(1)} fusion(bf16[85,2560]{1,0:T(8,128)(2,1)S(1)} %bitcast_dynamic-update-slice_fusion, bf16[2560,2048]{1,0:T(8,128)(2,1)S(1)} %bitcast.56), kind=kOutput, calls=%fused_computation.26 | convolution fusion | flops 891463680 | bytes 11269120 | tf_op jit(solution)/shard_map/dot_general | solution.py:45
  38.7 4.2 %copy.26 = bf16[5,17,2048]{1,0,2:T(8,128)(2,1)} copy(bf16[5,17,2048]{2,1,0:T(8,128)(2,1)S(1)} %reshape.27) | data formatting | bytes 696320 | tf_op jit(solution)/shard_map/reshape | solution.py:48
  42.9 5.9 %reshape.28 = bf16[8,2,10880]{2,1,0:T(2,128)(2,1)} reshape(bf16[2048,5,17]{2,1,0:T(8,128)(2,1)} %bitcast.57) | data formatting | bytes 696320
  48.8 8.5 %all-to-all-start = ((bf16[8,2,10880]{2,1,0:T(2,128)(2,1)}), bf16[8,2,10880]{2,1,0:T(2,128)(2,1)S(1)}, u32[]{:S(2)}, u32[]{:S(2)}) async-start(bf16[8,2,10880]{2,1,0:T(2,128)(2,1)} %reshape.28), calls=%async_computation | async-start | bytes 696320 | tf_op jit(solution)/shard_map/all_to_all | solution.py:55
  57.7 11.4 %all-to-all-done = bf16[8,2,10880]{2,1,0:T(2,128)(2,1)S(1)} async-done(((bf16[8,2,10880]{2,1,0:T(2,128)(2,1)}), bf16[8,2,10880]{2,1,0:T(2,128)(2,1)S(1)}, u32[]{:S(2)}, u32[]{:S(2)}) %all-to-all-start) | async-done | bytes 348192 | tf_op jit(solution)/shard_map/all_to_all | solution.py:55
  69.2 5.0 %reshape.29 = bf16[2048,5,17]{2,1,0:T(8,128)(2,1)} reshape(bf16[8,2,10880]{2,1,0:T(2,128)(2,1)S(1)} %all-to-all-done) | data formatting | bytes 696320
  74.2 4.2 %copy.28 = bf16[5,8,17,256]{3,2,1,0:T(8,128)(2,1)S(1)} copy(bf16[5,8,17,256]{2,0,3,1:T(8,128)(2,1)} %bitcast.58) | data formatting | bytes 696320 | tf_op jit(solution)/shard_map/all_to_all | solution.py:55
  78.5 0.8 copy.33
  79.3 12.0 %fusion.22 = bf16[5,127,256]{1,0,2:T(8,128)(2,1)S(1)} fusion(bf16[5,136,256]{1,0,2:T(8,128)(2,1)S(1)} %copy.33, f32[127,256]{0,1:T(8,128)S(1)} %copy.32, s32[127,256]{0,1:T(8,128)S(1)} %copy.31, f32[127,256]{0,1:T(8,128)S(1)} %copy.30, s32[127,256]{0,1:T(8,128)S(1)} %copy.29), kind=kOutput, calls=%fused_computation.28 | convolution fusion | flops 287568640 | bytes 1193472 | tf_op jit(solution)/shard_map/jlc,flc->fjc/dot_general | solution.py:58
  91.3 1.1 %copy.34 = bf16[5,127,256]{2,1,0:T(8,128)(2,1)} copy(bf16[5,127,256]{1,0,2:T(8,128)(2,1)S(1)} %fusion.22) | data formatting | bytes 650240 | tf_op jit(solution)/shard_map/convert_element_type | solution.py:59
  (40 shorter events, 2.9 us)
Async XLA Ops:
  1.5 18.1 %collective-permute-start.2 = (s32[512]{0:T(512)S(1)}, s32[512]{0:T(512)S(1)}, u32[]{:S(2)}, u32[]{:S(2)}) collective-permute-start(s32[512]{0:T(512)S(1)} %get-tuple-element.7), channel_id=1, source_target_pairs={{8,0},{16,8},{24,16},{32,24},{40,32},{48,40},{56,48},{64,56},{72,6... | collective-permute-start | bytes 6152 | tf_op jit(solution)/shard_map/ppermute | solution.py:10
  1.7 20.5 %collective-permute-start = (s32[512]{0:T(512)S(1)}, s32[512]{0:T(512)S(1)}, u32[]{:S(2)}, u32[]{:S(2)}) collective-permute-start(s32[512]{0:T(512)S(1)} %get-tuple-element.8), channel_id=1, source_target_pairs={{16,0},{24,8},{32,16},{40,24},{48,32},{56,40},{64,48},{72,56},{80,... | collective-permute-start | bytes 6152 | tf_op jit(solution)/shard_map/ppermute | solution.py:10
  2.4 21.7 %collective-permute-start.4 = (s32[512]{0:T(512)S(1)}, s32[512]{0:T(512)S(1)}, u32[]{:S(2)}, u32[]{:S(2)}) collective-permute-start(s32[512]{0:T(512)S(1)} %get-tuple-element.9), channel_id=1, source_target_pairs={{248,0},{0,8},{8,16},{16,24},{24,32},{32,40},{40,48},{48,56},{56,6... | collective-permute-start | bytes 6152 | tf_op jit(solution)/shard_map/ppermute | solution.py:10
  2.5 24.4 %collective-permute-start.6 = (s32[512]{0:T(512)S(1)}, s32[512]{0:T(512)S(1)}, u32[]{:S(2)}, u32[]{:S(2)}) collective-permute-start(s32[512]{0:T(512)S(1)} %get-tuple-element.5), channel_id=1, source_target_pairs={{240,0},{248,8},{0,16},{8,24},{16,32},{24,40},{32,48},{40,56},{48,... | collective-permute-start | bytes 6152 | tf_op jit(solution)/shard_map/ppermute | solution.py:10
  19.6 17.1 %slice-start = ((s8[10485760]{0:T(1024)(128)(4,1)}), s8[4194304]{0:T(1024)(128)(4,1)S(1)}, s32[]{:S(2)}) async-start(s8[10485760]{0:T(1024)(128)(4,1)} %bitcast.54), calls=%async_computation.1 | async-start | bytes 8388608
  21.0 15.6 %slice-start.1 = ((s8[10485760]{0:T(1024)(128)(4,1)}), s8[4194304]{0:T(1024)(128)(4,1)S(1)}, s32[]{:S(2)}) async-start(s8[10485760]{0:T(1024)(128)(4,1)} %bitcast.54), calls=%async_computation.2 | async-start | bytes 8388608
  21.1 8.5 %collective-permute-start.3 = (bf16[85,512]{1,0:T(8,128)(2,1)S(1)}, bf16[85,512]{1,0:T(8,128)(2,1)S(1)}, u32[]{:S(2)}, u32[]{:S(2)}) collective-permute-start(bf16[85,512]{1,0:T(8,128)(2,1)S(1)} %fusion.31), channel_id=1, source_target_pairs={{248,0},{0,8},{8,16},{16,24},{24,32},{32,40},{40,48},{48,56},{56,6... | collective-permute-start | bytes 261128 | tf_op jit(solution)/shard_map/ppermute | solution.py:10
  23.7 5.8 %collective-permute-start.1 = (bf16[85,512]{1,0:T(8,128)(2,1)S(1)}, bf16[85,512]{1,0:T(8,128)(2,1)S(1)}, u32[]{:S(2)}, u32[]{:S(2)}) collective-permute-start(bf16[85,512]{1,0:T(8,128)(2,1)S(1)} %fusion.30), channel_id=1, source_target_pairs={{240,0},{248,8},{0,16},{8,24},{16,32},{24,40},{32,48},{40,56},{48,... | collective-permute-start | bytes 261128 | tf_op jit(solution)/shard_map/ppermute | solution.py:10
  25.5 11.2 %slice-start.2 = ((s8[10485760]{0:T(1024)(128)(4,1)}), s8[2097152]{0:T(1024)(128)(4,1)S(1)}, s32[]{:S(2)}) async-start(s8[10485760]{0:T(1024)(128)(4,1)} %bitcast.54), calls=%async_computation.3 | async-start | bytes 4194304
  25.5 5.5 %collective-permute-start.5 = (bf16[85,512]{1,0:T(8,128)(2,1)S(1)}, bf16[85,512]{1,0:T(8,128)(2,1)S(1)}, u32[]{:S(2)}, u32[]{:S(2)}) collective-permute-start(bf16[85,512]{1,0:T(8,128)(2,1)S(1)} %fusion.34), channel_id=1, source_target_pairs={{8,0},{16,8},{24,16},{32,24},{40,32},{48,40},{56,48},{64,56},{72,6... | collective-permute-start | bytes 261128 | tf_op jit(solution)/shard_map/ppermute | solution.py:10
  28.5 8.1 %collective-permute-start.7 = (bf16[85,512]{1,0:T(8,128)(2,1)S(1)}, bf16[85,512]{1,0:T(8,128)(2,1)S(1)}, u32[]{:S(2)}, u32[]{:S(2)}) collective-permute-start(bf16[85,512]{1,0:T(8,128)(2,1)S(1)} %fusion.35), channel_id=1, source_target_pairs={{16,0},{24,8},{32,16},{40,24},{48,32},{56,40},{64,48},{72,56},{80,... | collective-permute-start | bytes 261128 | tf_op jit(solution)/shard_map/ppermute | solution.py:10
  38.6 18.7 %copy-start = (f32[127,256]{1,0:T(8,128)S(1)}, f32[127,256]{1,0:T(8,128)}, u32[]{:S(2)}) copy-start(f32[127,256]{1,0:T(8,128)} %param.11) | copy-start | bytes 390148
  38.6 18.9 %copy-start.1 = (s32[127,256]{1,0:T(8,128)S(1)}, s32[127,256]{1,0:T(8,128)}, u32[]{:S(2)}) copy-start(s32[127,256]{1,0:T(8,128)} %param.10) | copy-start | bytes 390148
  48.8 20.4 %all-to-all-start = ((bf16[8,2,10880]{2,1,0:T(2,128)(2,1)}), bf16[8,2,10880]{2,1,0:T(2,128)(2,1)S(1)}, u32[]{:S(2)}, u32[]{:S(2)}) async-start(bf16[8,2,10880]{2,1,0:T(2,128)(2,1)} %reshape.28), calls=%async_computation | async-start | bytes 696320 | tf_op jit(solution)/shard_map/all_to_all | solution.py:55
where the time goes:
time: 92.9 us; the launch traced here: 92.4 us
  local copies, waits for them, and re-layouts  24 us (26%)
  matrix products  21.2 us (23%)
  starting transfers between devices  18.1 us (19%)
  waiting for transfers between devices  17 us (18%)
  between operations  9.87 us (11%)
  other arithmetic  2.17 us (2%)
    dot_general x1, matrix products, local(): jnp.einsum('jlc,flc->fjc', interp, widened, precision=lax.Precision.HIGHEST)  12 us
    all_to_all x1, waiting for transfers between devices, local(): lax.all_to_all(horizontal, 'lev', split_axis=2, concat_axis=1, tiled=True)  11.4 us
    unnamed x21, local copies, waits for them, and re-layouts  11.2 us
    ppermute x8, starting transfers between devices, shifted(): return lax.ppermute(block, axis, route)  9.63 us
    all_to_all x1, starting transfers between devices, local(): lax.all_to_all(horizontal, 'lev', split_axis=2, concat_axis=1, tiled=True)  8.47 us
    dot_general x5, matrix products, select_cells(): jnp.dot(tile, picker, preferred_element_type=jnp.float32)  7.4 us
    ppermute x8, waiting for transfers between devices, shifted(): return lax.ppermute(block, axis, route)  5.53 us
    all_to_all x3, local copies, waits for them, and re-layouts, local(): lax.all_to_all(horizontal, 'lev', split_axis=2, concat_axis=1, tiled=True)  5.14 us
  transfers between devices with their start and end apart: 9, of which 2 were waited for; matrix products, arithmetic and copies ran while one was open for 11% of the time, Pallas kernels for 0%

commit v1 on v0

v1 whole, which is shorter than its diff:
```python
import functools

import jax
import jax.numpy as jnp
from jax import lax
from jax.experimental import pallas as pl
from jax.experimental.pallas import tpu as pltpu
from jax.sharding import PartitionSpec as P

MESH = pl.DeviceIdType.MESH
CHUNK = 256


def pick_rows(values, rows):
    return jnp.take_along_axis(values, rows, axis=0, mode="promise_in_bounds")


def kernel(
    groups,
    slabs,
    source_hbm,
    intersection_hbm,
    index_hbm,
    blocks_hbm,
    bracket_hbm,
    fraction_hbm,
    out_ref,
    source,
    intersection,
    index_map,
    weights,
    bracket_in,
    fraction_in,
    bracket,
    fraction,
    stacked,
    wanted,
    asked,
    picked,
    chosen,
    outbound,
    arrived,
    slab,
    total,
    local_sem,
    ask_send,
    ask_recv,
    value_send,
    value_recv,
    slab_send,
    slab_recv,
):
    group = lax.axis_index("horiz")
    place = lax.axis_index("lev")
    block_count = index_map.shape[0]
    depth = (block_count - 1) // 2
    fields, level_slab, tile_cells = source.shape
    rows = stacked.shape[0] // (tile_cells // CHUNK)
    even = level_slab - 1
    tail = fields * even
    columns = outbound.shape[2]
    offsets = [o for o in range(-depth, depth + 1) if o != 0]

    barrier = pltpu.get_barrier_semaphore()
    for offset in offsets:
        pl.semaphore_signal(
            barrier, inc=1, device_id={"horiz": lax.rem(group + offset + groups, groups)}, device_id_type=MESH
        )
    for step in range(1, slabs):
        pl.semaphore_signal(
            barrier, inc=1, device_id={"lev": lax.rem(place + step, slabs)}, device_id_type=MESH
        )

    loads = [
        pltpu.make_async_copy(src, dst, local_sem.at[n])
        for n, (src, dst) in enumerate(
            [
                (intersection_hbm, intersection),
                (index_hbm, index_map),
                (source_hbm, source),
                (bracket_hbm, bracket_in),
                (fraction_hbm, fraction_in),
                (blocks_hbm, weights),
            ]
        )
    ]
    for load in loads:
        load.start()
    loads[0].wait()
    loads[1].wait()

    for slot, offset in enumerate(range(-depth, depth + 1)):
        target = lax.rem(group + offset + groups, groups)
        row = jnp.zeros((1, index_map.shape[1]), jnp.int32)
        for block in range(block_count):
            row = row + jnp.where(intersection[block] == target, index_map[block : block + 1, :], 0)
        wanted[slot] = row

    pl.semaphore_wait(barrier, len(offsets) + slabs - 1)

    def ask(offset):
        slot = offset + depth
        return pltpu.make_async_remote_copy(
            src_ref=wanted.at[slot],
            dst_ref=asked.at[slot],
            send_sem=ask_send.at[slot],
            recv_sem=ask_recv.at[slot],
            device_id={"horiz": lax.rem(group + offset + groups, groups)},
            device_id_type=MESH,
        )

    def answer(offset):
        slot = offset + depth
        return pltpu.make_async_remote_copy(
            src_ref=picked.at[slot],
            dst_ref=chosen.at[slot],
            send_sem=value_send.at[slot],
            recv_sem=value_recv.at[slot],
            device_id={"horiz": lax.rem(group - offset + groups, groups)},
            device_id_type=MESH,
        )

    for offset in offsets:
        ask(offset).start()

    loads[2].wait()
    for chunk in range(tile_cells // CHUNK):
        cells = slice(chunk * CHUNK, (chunk + 1) * CHUNK)
        base = chunk * rows
        for field in range(fields):
            stacked[base + field * even : base + (field + 1) * even, :] = source[field, 0:even, cells]
        last = [source[field, even : even + 1, cells].astype(jnp.float32) for field in range(fields)]
        last.append(jnp.zeros((rows - tail - fields, CHUNK), jnp.float32))
        stacked[base + tail : base + rows, :] = jnp.concatenate(last, axis=0).astype(jnp.bfloat16)

    def select_cells(cell_ids):
        low = cell_ids & (CHUNK - 1)
        high = lax.shift_right_logical(cell_ids, CHUNK.bit_length() - 1)
        width = cell_ids.shape[1]
        picker = (
            (lax.broadcasted_iota(jnp.int32, (CHUNK, width), 0) == low).astype(jnp.float32).astype(jnp.bfloat16)
        )
        result = jnp.zeros((rows, width), jnp.float32)
        for chunk in range(tile_cells // CHUNK):
            part = jnp.dot(
                stacked[chunk * rows : (chunk + 1) * rows, :], picker, preferred_element_type=jnp.float32
            )
            result = jnp.where(high == chunk, part, result)
        return result.astype(jnp.bfloat16)

    chosen[depth] = select_cells(wanted[depth])
    for offset in offsets:
        slot = offset + depth
        ask(offset).wait_recv()
        picked[slot] = select_cells(asked[slot])
        answer(offset).start()

    loads[3].wait()
    loads[4].wait()
    levels_out = bracket_in.shape[0]
    bracket[bracket.shape[0] - 8 :, :] = jnp.zeros((8, columns), jnp.int32)
    fraction[fraction.shape[0] - 8 :, :] = jnp.zeros((8, columns), jnp.float32)
    bracket[0:levels_out, :] = bracket_in[...]
    fraction[0:levels_out, :] = fraction_in[...]
    total[...] = jnp.zeros_like(total)

    loads[5].wait()
    for offset in offsets:
        answer(offset).wait_recv()

    def deliver(step):
        return pltpu.make_async_remote_copy(
            src_ref=outbound.at[step],
            dst_ref=arrived.at[step],
            send_sem=slab_send.at[step],
            recv_sem=slab_recv.at[step],
            device_id={"lev": lax.rem(place + step, slabs)},
            device_id_type=MESH,
        )

    half = slabs // 2
    order = [half] + [s for d in range(half - 1, 0, -1) for s in (d, slabs - d)]
    positions = [
        jnp.minimum(lax.rem(intersection[b] - group + depth + groups, groups), block_count - 1)
        for b in range(block_count)
    ]
    for step in order + [0]:
        first = pl.multiple_of(lax.rem(place + step, slabs) * columns, columns)
        block = jnp.zeros((rows, columns), jnp.float32)
        for b in range(block_count):
            block = block + jnp.dot(
                chosen[positions[b]], weights[b, :, pl.ds(first, columns)], preferred_element_type=jnp.float32
            )
        if step == 0:
            arrived[0] = block.astype(jnp.bfloat16)
        else:
            outbound[step] = block.astype(jnp.bfloat16)
            deliver(step).start()

    for step in [0] + order:
        if step != 0:
            deliver(step).wait_recv()
        slab[...] = arrived[step].astype(jnp.float32)
        level0 = lax.rem(place - step + slabs, slabs) * level_slab

        for part in range(columns // 128):
            lanes = slice(part * 128, (part + 1) * 128)

            def mix(j, carry):
                out_rows = pl.ds(pl.multiple_of(j * 8, 8), 8)
                lower = bracket[out_rows, lanes] - level0
                upper = lower + 1
                share = fraction[out_rows, lanes]
                rest = 1.0 - share
                lower_tile, upper_tile = lower >> 3, upper >> 3
                lower_row, upper_row = lower & 7, upper & 7
                lower_last, upper_last = lower == even, upper == even
                for field in range(fields):
                    below = jnp.zeros((8, 128), jnp.float32)
                    above = jnp.zeros((8, 128), jnp.float32)
                    for tile in range(even // 8):
                        values = slab[field * even + tile * 8 : field * even + tile * 8 + 8, lanes]
                        below = jnp.where(lower_tile == tile, pick_rows(values, lower_row), below)
                        above = jnp.where(upper_tile == tile, pick_rows(values, upper_row), above)
                    last = slab[tail + field : tail + field + 1, lanes]
                    below = jnp.where(lower_last, last, below)
                    above = jnp.where(upper_last, last, above)
                    total[field, out_rows, lanes] += rest * below + share * above
                return carry

            lax.fori_loop(0, total.shape[1] // 8, mix, 0)

    out_ref[...] = total[:, 0:levels_out, :].astype(jnp.bfloat16)

    for offset in offsets:
        ask(offset).wait_send()
        answer(offset).wait_send()
    for step in order:
        deliver(step).wait_send()


def local(groups, slabs, source_state, intersection, index_map, blocks, bracket, fraction):
    fields, level_slab, tile_cells = source_state.shape
    block_count, width = index_map.shape
    levels_out, columns = bracket.shape
    rows = -(-fields * level_slab // 8) * 8
    out_rows = -(-levels_out // 8) * 8
    any_spec = pl.BlockSpec(memory_space=pl.ANY)
    dma = pltpu.SemaphoreType.DMA
    return pl.pallas_call(
        functools.partial(kernel, groups, slabs),
        out_shape=jax.ShapeDtypeStruct((fields, levels_out, columns), jnp.bfloat16),
        in_specs=[any_spec] * 6,
        out_specs=pl.BlockSpec(memory_space=pltpu.VMEM),
        scratch_shapes=[
            pltpu.VMEM(source_state.shape, jnp.bfloat16),
            pltpu.SMEM(intersection.shape, jnp.int32),
            pltpu.VMEM(index_map.shape, jnp.int32),
            pltpu.VMEM(blocks.shape, jnp.bfloat16),
            pltpu.VMEM(bracket.shape, jnp.int32),
            pltpu.VMEM(fraction.shape, jnp.float32),
            pltpu.VMEM((out_rows, columns), jnp.int32),
            pltpu.VMEM((out_rows, columns), jnp.float32),
            pltpu.VMEM((rows * (tile_cells // CHUNK), CHUNK), jnp.bfloat16),
            pltpu.VMEM((block_count, 1, width), jnp.int32),
            pltpu.VMEM((block_count, 1, width), jnp.int32),
            pltpu.VMEM((block_count, rows, width), jnp.bfloat16),
            pltpu.VMEM((block_count, rows, width), jnp.bfloat16),
            pltpu.VMEM((slabs, rows, columns), jnp.bfloat16),
            pltpu.VMEM((slabs, rows, columns), jnp.bfloat16),
            pltpu.VMEM((rows, columns), jnp.float32),
            pltpu.VMEM((fields, out_rows, columns), jnp.float32),
            dma((6,)),
            dma((block_count,)),
            dma((block_count,)),
            dma((block_count,)),
            dma((block_count,)),
            dma((slabs,)),
            dma((slabs,)),
        ],
        compiler_params=pltpu.CompilerParams(
            collective_id=0, has_side_effects=True, vmem_limit_bytes=56 * 1024 * 1024
        ),
        name="regrid",
    )(source_state, intersection, index_map, blocks, bracket, fraction)


def solution(mesh):
    in_specs = (
        P(None, "lev", "horiz"),
        P("horiz"),
        P("horiz", None),
        P("horiz", None, None),
        P(None, ("horiz", "lev")),
        P(None, ("horiz", "lev")),
    )
    out_specs = P(None, None, ("horiz", "lev"))
    body = functools.partial(local, mesh.shape["horiz"], mesh.shape["lev"])
    return jax.shard_map(body, mesh=mesh, in_specs=in_specs, out_specs=out_specs, check_vma=False)
```

time: 92.9 us -> 34.2 us (0.37)
  the two profiles are of different devices: /device:TPU:30 before, /device:TPU:54 now
where the time goes in v1:
time: 34.2 us; the launch traced here: 34.1 us
  Pallas kernels  32.3 us (94%)
  local copies, waits for them, and re-layouts  1.72 us (5%)
    pallas_call x1, Pallas kernels, local(): pl.pallas_call(functools.partial(kernel, groups, slabs), out_shape=jax.Sh...  32.3 us
    unnamed x1, local copies, waits for them, and re-layouts  1.72 us

profile of v1, /device:TPU:54, one launch (start us, length us, event | category | flops | bytes accessed | tf_op | source)
XLA Modules:
  0.0 34.1 jit_solution(7650117110113336734)
XLA Ops:
  0.0 32.3 %regrid.1 = bf16[5,127,256]{2,1,0:T(8,128)(2,1)} custom-call(bf16[5,17,4096]{2,1,0:T(8,128)(2,1)} %source_hbm.1, s32[5]{0:T(128)} %intersection_hbm.1, s32[5,512]{1,0:T(8,128)} %index_hbm.1, bf16[5,512,2048]{2,1,0:T(8,128)(2,1)} %blocks_hbm.1, s32[127,256]{1,0:T(8,128)} %bracket_hbm.1, f32[127,256]{1,0:T(8,128)} %fraction_hbm.1), custom_call_target="tpu_custom_call" | custom-call | tf_op jit(solution)/shard_map/regrid/pallas_call | solution.py:250
  32.4 1.7 %copy.8 = bf16[5,127,256]{2,1,0:T(8,128)(2,1)} copy(bf16[5,127,256]{2,1,0:T(8,128)(2,1)} %regrid.1) | data formatting | bytes 650240

commit v2 on v1

v2 whole, which is shorter than its diff:
```python
import functools

import jax
import jax.numpy as jnp
from jax import lax
from jax.experimental import pallas as pl
from jax.experimental.pallas import tpu as pltpu
from jax.sharding import PartitionSpec as P

MESH = pl.DeviceIdType.MESH
CHUNK = 256
TILE = 8


def pick_rows(values, rows):
    return jnp.take_along_axis(values, rows, axis=0, mode="promise_in_bounds")


def plan(fields, level_slab):
    tiles = level_slab // TILE
    odd = level_slab - tiles * TILE
    parts = []
    for tile in range(tiles):
        odd_rows = fields * odd if tile == tiles - 1 else 0
        parts.append((tile, fields * TILE, odd_rows, -(-(fields * TILE + odd_rows) // TILE) * TILE))
    return parts, odd


def kernel(
    groups,
    slabs,
    source_hbm,
    intersection_hbm,
    index_hbm,
    blocks_hbm,
    bracket_hbm,
    fraction_hbm,
    out_ref,
    source,
    intersection,
    index_map,
    weights,
    bracket_in,
    fraction_in,
    bracket,
    fraction,
    stacked,
    wanted,
    asked,
    picked,
    chosen,
    outbound,
    arrived,
    slab,
    total,
    local_sem,
    ask_send,
    ask_recv,
    value_send,
    value_recv,
    slab_send,
    slab_recv,
    rising,
    falling,
):
    group = lax.axis_index("horiz")
    place = lax.axis_index("lev")
    block_count = index_map.shape[0]
    depth = (block_count - 1) // 2
    fields, level_slab, tile_cells = source.shape
    chunks = tile_cells // CHUNK
    columns = bracket.shape[1]
    levels_out = bracket_in.shape[0]
    parts, odd = plan(fields, level_slab)
    tiles = len(parts)
    offsets = [sign * d for d in range(1, depth + 1) for sign in (-1, 1)]

    barrier = pltpu.get_barrier_semaphore()
    for offset in reversed(offsets):
        pl.semaphore_signal(
            barrier, inc=1, device_id={"horiz": lax.rem(group + offset + groups, groups)}, device_id_type=MESH
        )
    higher, lower_place = lax.rem(place + 1, slabs), lax.rem(place + slabs - 1, slabs)
    for neighbour in (higher, lower_place):
        pl.semaphore_signal(barrier, inc=1, device_id={"lev": neighbour}, device_id_type=MESH)

    loads = [
        pltpu.make_async_copy(src, dst, local_sem.at[n])
        for n, (src, dst) in enumerate(
            [
                (intersection_hbm, intersection),
                (index_hbm, index_map),
                (source_hbm, source),
                (bracket_hbm, bracket_in),
                (fraction_hbm, fraction_in),
                (blocks_hbm, weights),
            ]
        )
    ]
    for load in loads:
        load.start()
    loads[0].wait()
    loads[1].wait()

    for slot, offset in enumerate(range(-depth, depth + 1)):
        target = lax.rem(group + offset + groups, groups)
        row = jnp.zeros((1, index_map.shape[1]), jnp.int32)
        for block in range(block_count):
            row = row + jnp.where(intersection[block] == target, index_map[block : block + 1, :], 0)
        wanted[slot] = row

    pl.semaphore_wait(barrier, len(offsets) + 2)

    def ask(offset):
        slot = offset + depth
        return pltpu.make_async_remote_copy(
            src_ref=wanted.at[slot],
            dst_ref=asked.at[slot],
            send_sem=ask_send.at[slot],
            recv_sem=ask_recv.at[slot],
            device_id={"horiz": lax.rem(group + offset + groups, groups)},
            device_id_type=MESH,
        )

    def answer(part, offset):
        slot = offset + depth
        return pltpu.make_async_remote_copy(
            src_ref=picked[part].at[slot],
            dst_ref=chosen[part].at[slot],
            send_sem=value_send.at[part, slot],
            recv_sem=value_recv.at[part, slot],
            device_id={"horiz": lax.rem(group - offset + groups, groups)},
            device_id_type=MESH,
        )

    def deliver(part, step):
        return pltpu.make_async_remote_copy(
            src_ref=outbound[part].at[step],
            dst_ref=arrived[part].at[step],
            send_sem=slab_send.at[part, step],
            recv_sem=slab_recv.at[part, step],
            device_id={"lev": lax.rem(place + step, slabs)},
            device_id_type=MESH,
        )

    rounds = slabs // 2 - 1

    def tell(turn):
        pl.semaphore_signal(rising.at[turn], inc=1, device_id={"lev": higher}, device_id_type=MESH)
        pl.semaphore_signal(falling.at[turn], inc=1, device_id={"lev": lower_place}, device_id_type=MESH)

    def hear(turn):
        pl.semaphore_wait(rising.at[turn], 1)
        pl.semaphore_wait(falling.at[turn], 1)
        if turn + 1 < rounds:
            tell(turn + 1)

    for offset in reversed(offsets):
        ask(offset).start()
    tell(0)

    loads[2].wait()
    for part, (tile, full_rows, odd_rows, rows) in enumerate(parts):
        for chunk in range(chunks):
            cells = slice(chunk * CHUNK, (chunk + 1) * CHUNK)
            base = chunk * rows
            for field in range(fields):
                stacked[part][base + field * TILE : base + (field + 1) * TILE, :] = source[
                    field, tile * TILE : (tile + 1) * TILE, cells
                ]
            if odd_rows:
                last = [source[field, tiles * TILE :, cells].astype(jnp.float32) for field in range(fields)]
                last.append(jnp.zeros((rows - full_rows - odd_rows, CHUNK), jnp.float32))
                stacked[part][base + full_rows : base + rows, :] = jnp.concatenate(last, axis=0).astype(
                    jnp.bfloat16
                )

    def select_cells(part, cell_ids, result_ref):
        rows = parts[part][3]
        for piece in range(cell_ids.shape[1] // CHUNK):
            cells = slice(piece * CHUNK, (piece + 1) * CHUNK)
            low = cell_ids[:, cells] & (CHUNK - 1)
            high = lax.shift_right_logical(cell_ids[:, cells], CHUNK.bit_length() - 1)
            picker = (
                (lax.broadcasted_iota(jnp.int32, (CHUNK, CHUNK), 0) == low).astype(jnp.float32).astype(jnp.bfloat16)
            )
            found = jnp.dot(stacked[part][...], picker, preferred_element_type=jnp.float32)
            result = jnp.zeros((rows, CHUNK), jnp.float32)
            for chunk in range(chunks):
                result = jnp.where(high == chunk, found[chunk * rows : (chunk + 1) * rows], result)
            result_ref[:, cells] = result.astype(jnp.bfloat16)

    for part in range(tiles):
        select_cells(part, wanted[depth], chosen[part].at[depth])
    loads[3].wait()
    loads[4].wait()
    bracket[bracket.shape[0] - TILE :, :] = jnp.zeros((TILE, columns), jnp.int32)
    fraction[fraction.shape[0] - TILE :, :] = jnp.zeros((TILE, columns), jnp.float32)
    bracket[0:levels_out, :] = bracket_in[...]
    fraction[0:levels_out, :] = fraction_in[...]

    for part in range(tiles):
        for offset in offsets:
            slot = offset + depth
            if part == 0:
                ask(offset).wait_recv()
            select_cells(part, asked[slot], picked[part].at[slot])
            answer(part, offset).start()
        if part < rounds:
            hear(part)

    half = slabs // 2
    order = [half] + [s for d in range(half - 1, 0, -1) for s in (d, slabs - d)]
    positions = [
        jnp.minimum(lax.rem(intersection[b] - group + depth + groups, groups), block_count - 1)
        for b in range(block_count)
    ]
    loads[5].wait()
    for part in range(tiles):
        rows = parts[part][3]
        for offset in offsets:
            answer(part, offset).wait_recv()
        if part == 0:
            for turn in range(min(tiles, rounds), rounds):
                hear(turn)
        for step in order + [0]:
            first = pl.multiple_of(lax.rem(place + step, slabs) * columns, columns)
            block = jnp.zeros((rows, columns), jnp.float32)
            for b in range(block_count):
                block = block + jnp.dot(
                    chosen[part][positions[b]],
                    weights[b, :, pl.ds(first, columns)],
                    preferred_element_type=jnp.float32,
                )
            if step == 0:
                arrived[part][0] = block.astype(jnp.bfloat16)
            else:
                outbound[part][step] = block.astype(jnp.bfloat16)
                deliver(part, step).start()

    def blend(pairs, start):
        for part, step in pairs:
            slab[part][step] = arrived[part][step].astype(jnp.float32)

        def mix(j, carry):
            out_rows = pl.ds(pl.multiple_of(j * TILE, TILE), TILE)
            for piece in range(columns // 128):
                lanes = slice(piece * 128, (piece + 1) * 128)
                share = fraction[out_rows, lanes]
                rest = 1.0 - share
                below = [jnp.zeros((TILE, 128), jnp.float32)] * fields
                above = [jnp.zeros((TILE, 128), jnp.float32)] * fields
                for part, step in pairs:
                    tile, full_rows, odd_rows, rows = parts[part]
                    level0 = lax.rem(place - step + slabs, slabs) * level_slab
                    lower = bracket[out_rows, lanes] - level0
                    upper = lower + 1
                    in_lower, in_upper = (lower >> 3) == tile, (upper >> 3) == tile
                    lower_row, upper_row = lower & (TILE - 1), upper & (TILE - 1)
                    for field in range(fields):
                        values = slab[part][step, field * TILE : (field + 1) * TILE, lanes]
                        below[field] = jnp.where(in_lower, pick_rows(values, lower_row), below[field])
                        above[field] = jnp.where(in_upper, pick_rows(values, upper_row), above[field])
                    if odd_rows:
                        for extra in range(odd):
                            at_lower = lower == tiles * TILE + extra
                            at_upper = upper == tiles * TILE + extra
                            for field in range(fields):
                                row = full_rows + field * odd + extra
                                last = slab[part][step, row : row + 1, lanes]
                                below[field] = jnp.where(at_lower, last, below[field])
                                above[field] = jnp.where(at_upper, last, above[field])
                for field in range(fields):
                    mixed = rest * below[field] + share * above[field]
                    if start:
                        total[field, out_rows, lanes] = mixed
                    else:
                        total[field, out_rows, lanes] += mixed
            return carry

        lax.fori_loop(0, total.shape[1] // TILE, mix, 0)

    blend([(part, 0) for part in range(tiles)], True)
    ordered = [order[0:3]] + [order[n : n + 2] for n in range(3, len(order), 2)]
    for part in range(tiles):
        for steps in ordered:
            for step in steps:
                deliver(part, step).wait_recv()
            blend([(part, step) for step in steps], False)

    out_ref[...] = total[:, 0:levels_out, :].astype(jnp.bfloat16)

    for offset in offsets:
        ask(offset).wait_send()
        for part in range(tiles):
            answer(part, offset).wait_send()
    for step in order:
        for part in range(tiles):
            deliver(part, step).wait_send()


def local(groups, slabs, source_state, intersection, index_map, blocks, bracket, fraction):
    fields, level_slab, tile_cells = source_state.shape
    block_count, width = index_map.shape
    levels_out, columns = bracket.shape
    out_rows = -(-levels_out // TILE) * TILE
    chunks = tile_cells // CHUNK
    parts, _ = plan(fields, level_slab)
    rounds = slabs // 2 - 1
    any_spec = pl.BlockSpec(memory_space=pl.ANY)
    dma = pltpu.SemaphoreType.DMA

    def per_part(shape_of, dtype=jnp.bfloat16):
        return [pltpu.VMEM(shape_of(rows), dtype) for *_, rows in parts]

    return pl.pallas_call(
        functools.partial(kernel, groups, slabs),
        out_shape=pltpu.VMEM((fields, levels_out, columns), jnp.bfloat16),
        in_specs=[any_spec] * 6,
        out_specs=pl.BlockSpec(memory_space=pltpu.VMEM),
        scratch_shapes=[
            pltpu.VMEM(source_state.shape, jnp.bfloat16),
            pltpu.SMEM(intersection.shape, jnp.int32),
            pltpu.VMEM(index_map.shape, jnp.int32),
            pltpu.VMEM(blocks.shape, jnp.bfloat16),
            pltpu.VMEM(bracket.shape, jnp.int32),
            pltpu.VMEM(fraction.shape, jnp.float32),
            pltpu.VMEM((out_rows, columns), jnp.int32),
            pltpu.VMEM((out_rows, columns), jnp.float32),
            per_part(lambda rows: (rows * chunks, CHUNK)),
            pltpu.VMEM((block_count, 1, width), jnp.int32),
            pltpu.VMEM((block_count, 1, width), jnp.int32),
            per_part(lambda rows: (block_count, rows, width)),
            per_part(lambda rows: (block_count, rows, width)),
            per_part(lambda rows: (slabs, rows, columns)),
            per_part(lambda rows: (slabs, rows, columns)),
            per_part(lambda rows: (slabs, rows, columns), jnp.float32),
            pltpu.VMEM((fields, out_rows, columns), jnp.float32),
            dma((6,)),
            dma((block_count,)),
            dma((block_count,)),
            dma((len(parts), block_count)),
            dma((len(parts), block_count)),
            dma((len(parts), slabs)),
            dma((len(parts), slabs)),
            pltpu.SemaphoreType.REGULAR((rounds,)),
            pltpu.SemaphoreType.REGULAR((rounds,)),
        ],
        compiler_params=pltpu.CompilerParams(
            collective_id=0, has_side_effects=True, vmem_limit_bytes=56 * 1024 * 1024
        ),
        name="regrid",
    )(source_state, intersection, index_map, blocks, bracket, fraction)


def solution(mesh):
    in_specs = (
        P(None, "lev", "horiz"),
        P("horiz"),
        P("horiz", None),
        P("horiz", None, None),
        P(None, ("horiz", "lev")),
        P(None, ("horiz", "lev")),
    )
    out_specs = P(None, None, ("horiz", "lev"))
    body = functools.partial(local, mesh.shape["horiz"], mesh.shape["lev"])
    return jax.shard_map(body, mesh=mesh, in_specs=in_specs, out_specs=out_specs, check_vma=False)
```

time: 34.2 us -> 33.6 us (0.982)
  the two profiles are of different devices: /device:TPU:54 before, /device:TPU:1 now
where the time goes in v2:
time: 33.6 us; the launch traced here: 33.5 us
  Pallas kernels  32.8 us (98%)
  local copies, waits for them, and re-layouts  0.73 us (2%)
    pallas_call x1, Pallas kernels, local(): pl.pallas_call(functools.partial(kernel, groups, slabs), out_shape=pltpu....  32.8 us
    unnamed x1, local copies, waits for them, and re-layouts  0.73 us

profile of v2, /device:TPU:1, one launch (start us, length us, event | category | flops | bytes accessed | tf_op | source)
XLA Modules:
  0.0 33.5 jit_solution(2132320995074128901)
XLA Ops:
  0.0 32.8 %regrid.1 = bf16[5,127,256]{2,1,0:T(8,128)(2,1)S(1)} custom-call(bf16[5,17,4096]{2,1,0:T(8,128)(2,1)} %source_hbm.1, s32[5]{0:T(128)} %intersection_hbm.1, s32[5,512]{1,0:T(8,128)} %index_hbm.1, bf16[5,512,2048]{2,1,0:T(8,128)(2,1)} %blocks_hbm.1, s32[127,256]{1,0:T(8,128)} %bracket_hbm.1, f32[127,256]{1,0:T(8,128)} %fraction_hbm.1), custom_call_target="tpu_custom_call" | custom-call | tf_op jit(solution)/shard_map/regrid/pallas_call | solution.py:316
  32.8 0.7 %copy.8 = bf16[5,127,256]{2,1,0:T(8,128)(2,1)} copy(bf16[5,127,256]{2,1,0:T(8,128)(2,1)S(1)} %regrid.1) | data formatting | bytes 650240

commit v3 on v2

--- a/solution.py
+++ b/solution.py
@@ -19,11 +19,13 @@
 def plan(fields, level_slab):
     tiles = level_slab // TILE
     odd = level_slab - tiles * TILE
+    groups = [(0,)] + [tuple(range(f, min(f + 2, fields))) for f in range(1, fields, 2)]
     parts = []
-    for tile in range(tiles):
-        odd_rows = fields * odd if tile == tiles - 1 else 0
-        parts.append((tile, fields * TILE, odd_rows, -(-(fields * TILE + odd_rows) // TILE) * TILE))
-    return parts, odd
+    for number, members in enumerate(groups):
+        full_rows = len(members) * tiles * TILE
+        odd_rows = fields * odd if number == 0 else 0
+        parts.append((members, full_rows, odd_rows, -(-(full_rows + odd_rows) // TILE) * TILE))
+    return parts, tiles, odd
 
 
 def kernel(
@@ -71,12 +73,11 @@
     chunks = tile_cells // CHUNK
     columns = bracket.shape[1]
     levels_out = bracket_in.shape[0]
-    parts, odd = plan(fields, level_slab)
-    tiles = len(parts)
-    offsets = [sign * d for d in range(1, depth + 1) for sign in (-1, 1)]
+    parts, tiles, odd = plan(fields, level_slab)
+    offsets = list(range(1, depth + 1)) + list(range(-depth, 0))
 
     barrier = pltpu.get_barrier_semaphore()
-    for offset in reversed(offsets):
+    for offset in offsets:
         pl.semaphore_signal(
             barrier, inc=1, device_id={"horiz": lax.rem(group + offset + groups, groups)}, device_id_type=MESH
         )
@@ -155,18 +156,18 @@
         if turn + 1 < rounds:
             tell(turn + 1)
 
-    for offset in reversed(offsets):
+    for offset in offsets:
         ask(offset).start()
     tell(0)
 
     loads[2].wait()
-    for part, (tile, full_rows, odd_rows, rows) in enumerate(parts):
+    for part, (members, full_rows, odd_rows, rows) in enumerate(parts):
         for chunk in range(chunks):
             cells = slice(chunk * CHUNK, (chunk + 1) * CHUNK)
             base = chunk * rows
-            for field in range(fields):
-                stacked[part][base + field * TILE : base + (field + 1) * TILE, :] = source[
-                    field, tile * TILE : (tile + 1) * TILE, cells
+            for n, field in enumerate(members):
+                stacked[part][base + n * tiles * TILE : base + (n + 1) * tiles * TILE, :] = source[
+                    field, 0 : tiles * TILE, cells
                 ]
             if odd_rows:
                 last = [source[field, tiles * TILE :, cells].astype(jnp.float32) for field in range(fields)]
@@ -190,7 +191,7 @@
                 result = jnp.where(high == chunk, found[chunk * rows : (chunk + 1) * rows], result)
             result_ref[:, cells] = result.astype(jnp.bfloat16)
 
-    for part in range(tiles):
+    for part in range(len(parts)):
         select_cells(part, wanted[depth], chosen[part].at[depth])
     loads[3].wait()
     loads[4].wait()
@@ -199,7 +200,7 @@
     bracket[0:levels_out, :] = bracket_in[...]
     fraction[0:levels_out, :] = fraction_in[...]
 
-    for part in range(tiles):
+    for part in range(len(parts)):
         for offset in offsets:
             slot = offset + depth
             if part == 0:
@@ -216,12 +217,12 @@
         for b in range(block_count)
     ]
     loads[5].wait()
-    for part in range(tiles):
+    for part in range(len(parts)):
         rows = parts[part][3]
         for offset in offsets:
             answer(part, offset).wait_recv()
         if part == 0:
-            for turn in range(min(tiles, rounds), rounds):
+            for turn in range(min(len(parts), rounds), rounds):
                 hear(turn)
         for step in order + [0]:
             first = pl.multiple_of(lax.rem(place + step, slabs) * columns, columns)
@@ -238,8 +239,10 @@
                 outbound[part][step] = block.astype(jnp.bfloat16)
                 deliver(part, step).start()
 
-    def blend(pairs, start):
-        for part, step in pairs:
+    def blend(part, steps, start):
+        members, full_rows, odd_rows, rows = parts[part]
+        touched = range(fields) if odd_rows else members
+        for step in steps:
             slab[part][step] = arrived[part][step].astype(jnp.float32)
 
         def mix(j, carry):
@@ -248,19 +251,21 @@
                 lanes = slice(piece * 128, (piece + 1) * 128)
                 share = fraction[out_rows, lanes]
                 rest = 1.0 - share
-                below = [jnp.zeros((TILE, 128), jnp.float32)] * fields
-                above = [jnp.zeros((TILE, 128), jnp.float32)] * fields
-                for part, step in pairs:
-                    tile, full_rows, odd_rows, rows = parts[part]
+                below = {field: jnp.zeros((TILE, 128), jnp.float32) for field in touched}
+                above = {field: jnp.zeros((TILE, 128), jnp.float32) for field in touched}
+                for step in steps:
                     level0 = lax.rem(place - step + slabs, slabs) * level_slab
                     lower = bracket[out_rows, lanes] - level0
                     upper = lower + 1
-                    in_lower, in_upper = (lower >> 3) == tile, (upper >> 3) == tile
+                    lower_tile, upper_tile = lower >> 3, upper >> 3
                     lower_row, upper_row = lower & (TILE - 1), upper & (TILE - 1)
-                    for field in range(fields):
-                        values = slab[part][step, field * TILE : (field + 1) * TILE, lanes]
-                        below[field] = jnp.where(in_lower, pick_rows(values, lower_row), below[field])
-                        above[field] = jnp.where(in_upper, pick_rows(values, upper_row), above[field])
+                    for tile in range(tiles):
+                        in_lower, in_upper = lower_tile == tile, upper_tile == tile
+                        for n, field in enumerate(members):
+                            row = (n * tiles + tile) * TILE
+                            values = slab[part][step, row : row + TILE, lanes]
+                            below[field] = jnp.where(in_lower, pick_rows(values, lower_row), below[field])
+                            above[field] = jnp.where(in_upper, pick_rows(values, upper_row), above[field])
                     if odd_rows:
                         for extra in range(odd):
                             at_lower = lower == tiles * TILE + extra
@@ -270,7 +275,7 @@
                                 last = slab[part][step, row : row + 1, lanes]
                                 below[field] = jnp.where(at_lower, last, below[field])
                                 above[field] = jnp.where(at_upper, last, above[field])
-                for field in range(fields):
+                for field in touched:
                     mixed = rest * below[field] + share * above[field]
                     if start:
                         total[field, out_rows, lanes] = mixed
@@ -280,22 +285,24 @@
 
         lax.fori_loop(0, total.shape[1] // TILE, mix, 0)
 
-    blend([(part, 0) for part in range(tiles)], True)
-    ordered = [order[0:3]] + [order[n : n + 2] for n in range(3, len(order), 2)]
-    for part in range(tiles):
-        for steps in ordered:
+    for part in range(len(parts)):
+        if part < len(parts) - 1:
+            turns = [order]
+        else:
+            turns = [order[0:3]] + [order[n : n + 2] for n in range(3, len(order), 2)]
+        for n, steps in enumerate(turns):
             for step in steps:
                 deliver(part, step).wait_recv()
-            blend([(part, step) for step in steps], False)
+            blend(part, ([0] if n == 0 else []) + steps, part == 0)
 
     out_ref[...] = total[:, 0:levels_out, :].astype(jnp.bfloat16)
 
     for offset in offsets:
         ask(offset).wait_send()
-        for part in range(tiles):
+        for part in range(len(parts)):
             answer(part, offset).wait_send()
     for step in order:
-        for part in range(tiles):
+        for part in range(len(parts)):
             deliver(part, step).wait_send()
 
 
@@ -305,7 +312,7 @@
     levels_out, columns = bracket.shape
     out_rows = -(-levels_out // TILE) * TILE
     chunks = tile_cells // CHUNK
-    parts, _ = plan(fields, level_slab)
+    parts, _, _ = plan(fields, level_slab)
     rounds = slabs // 2 - 1
     any_spec = pl.BlockSpec(memory_space=pl.ANY)
     dma = pltpu.SemaphoreType.DMA

time: 33.6 us -> 33.9 us (level)
  the two profiles are of different devices: /device:TPU:1 before, /device:TPU:32 now
where the time goes in v3:
time: 33.9 us; the launch traced here: 33.8 us
  Pallas kernels  33.1 us (98%)
  local copies, waits for them, and re-layouts  0.73 us (2%)
    pallas_call x1, Pallas kernels, local(): pl.pallas_call(functools.partial(kernel, groups, slabs), out_shape=pltpu....  33.1 us
    unnamed x1, local copies, waits for them, and re-layouts  0.73 us

profile of v3, /device:TPU:32, one launch (start us, length us, event | category | flops | bytes accessed | tf_op | source)
XLA Modules:
  0.0 33.8 jit_solution(13831568508740338911)
XLA Ops:
  0.0 33.1 %regrid.1 = bf16[5,127,256]{2,1,0:T(8,128)(2,1)S(1)} custom-call(bf16[5,17,4096]{2,1,0:T(8,128)(2,1)} %source_hbm.1, s32[5]{0:T(128)} %intersection_hbm.1, s32[5,512]{1,0:T(8,128)} %index_hbm.1, bf16[5,512,2048]{2,1,0:T(8,128)(2,1)} %blocks_hbm.1, s32[127,256]{1,0:T(8,128)} %bracket_hbm.1, f32[127,256]{1,0:T(8,128)} %fraction_hbm.1), custom_call_target="tpu_custom_call" | custom-call | tf_op jit(solution)/shard_map/regrid/pallas_call | solution.py:323
  33.1 0.7 %copy.8 = bf16[5,127,256]{2,1,0:T(8,128)(2,1)} copy(bf16[5,127,256]{2,1,0:T(8,128)(2,1)S(1)} %regrid.1) | data formatting | bytes 650240

commit v4 on v3

v4 whole, which is shorter than its diff:
```python
import functools

import jax
import jax.numpy as jnp
from jax import lax
from jax.experimental import pallas as pl
from jax.experimental.pallas import tpu as pltpu
from jax.sharding import PartitionSpec as P

MESH = pl.DeviceIdType.MESH
CHUNK = 256
TILE = 8


def pick_rows(values, rows):
    return jnp.take_along_axis(values, rows, axis=0, mode="promise_in_bounds")


def kernel(
    groups,
    slabs,
    source_hbm,
    intersection_hbm,
    index_hbm,
    blocks_hbm,
    bracket_hbm,
    fraction_hbm,
    out_ref,
    source,
    intersection,
    index_map,
    weights,
    bracket_in,
    fraction_in,
    bracket,
    fraction,
    stacked,
    wanted,
    asked,
    picked,
    chosen,
    outbound,
    arrived,
    slab,
    total,
    local_sem,
    ask_send,
    ask_recv,
    value_send,
    value_recv,
    slab_send,
    slab_recv,
    rising,
    falling,
):
    group = lax.axis_index("horiz")
    place = lax.axis_index("lev")
    block_count = index_map.shape[0]
    depth = (block_count - 1) // 2
    fields, level_slab, tile_cells = source.shape
    chunks = tile_cells // CHUNK
    columns = bracket.shape[1]
    levels_out = bracket_in.shape[0]
    tiles = level_slab // TILE
    odd = level_slab - tiles * TILE
    even = tiles * TILE
    full_rows = fields * even
    rows = stacked.shape[0] // chunks
    offsets = list(range(1, depth + 1)) + list(range(-depth, 0))

    barrier = pltpu.get_barrier_semaphore()
    for offset in offsets:
        pl.semaphore_signal(
            barrier, inc=1, device_id={"horiz": lax.rem(group + offset + groups, groups)}, device_id_type=MESH
        )
    higher, lower_place = lax.rem(place + 1, slabs), lax.rem(place + slabs - 1, slabs)
    for neighbour in (higher, lower_place):
        pl.semaphore_signal(barrier, inc=1, device_id={"lev": neighbour}, device_id_type=MESH)

    loads = [
        pltpu.make_async_copy(src, dst, local_sem.at[n])
        for n, (src, dst) in enumerate(
            [
                (intersection_hbm, intersection),
                (index_hbm, index_map),
                (source_hbm, source),
                (bracket_hbm, bracket_in),
                (fraction_hbm, fraction_in),
                (blocks_hbm, weights),
            ]
        )
    ]
    for load in loads:
        load.start()
    loads[0].wait()
    loads[1].wait()

    for slot, offset in enumerate(range(-depth, depth + 1)):
        target = lax.rem(group + offset + groups, groups)
        row = jnp.zeros((1, index_map.shape[1]), jnp.int32)
        for block in range(block_count):
            row = row + jnp.where(intersection[block] == target, index_map[block : block + 1, :], 0)
        wanted[slot] = row

    pl.semaphore_wait(barrier, len(offsets) + 2)

    def ask(offset):
        slot = offset + depth
        return pltpu.make_async_remote_copy(
            src_ref=wanted.at[slot],
            dst_ref=asked.at[slot],
            send_sem=ask_send.at[slot],
            recv_sem=ask_recv.at[slot],
            device_id={"horiz": lax.rem(group + offset + groups, groups)},
            device_id_type=MESH,
        )

    def answer(offset):
        slot = offset + depth
        return pltpu.make_async_remote_copy(
            src_ref=picked.at[slot],
            dst_ref=chosen.at[slot],
            send_sem=value_send.at[slot],
            recv_sem=value_recv.at[slot],
            device_id={"horiz": lax.rem(group - offset + groups, groups)},
            device_id_type=MESH,
        )

    def deliver(target):
        return pltpu.make_async_remote_copy(
            src_ref=outbound.at[target],
            dst_ref=arrived.at[place],
            send_sem=slab_send.at[target],
            recv_sem=slab_recv.at[place],
            device_id={"lev": target},
            device_id_type=MESH,
        )

    def await_slab(origin):
        pltpu.make_async_remote_copy(
            src_ref=outbound.at[origin],
            dst_ref=arrived.at[origin],
            send_sem=slab_send.at[origin],
            recv_sem=slab_recv.at[origin],
            device_id={"lev": origin},
            device_id_type=MESH,
        ).wait_recv()

    rounds = slabs // 2 - 1

    def tell(turn):
        pl.semaphore_signal(rising.at[turn], inc=1, device_id={"lev": higher}, device_id_type=MESH)
        pl.semaphore_signal(falling.at[turn], inc=1, device_id={"lev": lower_place}, device_id_type=MESH)

    def hear(turn):
        pl.semaphore_wait(rising.at[turn], 1)
        pl.semaphore_wait(falling.at[turn], 1)
        if turn + 1 < rounds:
            tell(turn + 1)

    for offset in offsets:
        ask(offset).start()
    tell(0)

    loads[2].wait()
    for chunk in range(chunks):
        cells = slice(chunk * CHUNK, (chunk + 1) * CHUNK)
        base = chunk * rows
        for field in range(fields):
            stacked[base + field * even : base + (field + 1) * even, :] = source[field, 0:even, cells]
        last = [source[field, even:, cells].astype(jnp.float32) for field in range(fields)]
        last.append(jnp.zeros((rows - full_rows - fields * odd, CHUNK), jnp.float32))
        stacked[base + full_rows : base + rows, :] = jnp.concatenate(last, axis=0).astype(jnp.bfloat16)

    def select_cells(cell_ids, result_ref):
        for piece in range(cell_ids.shape[1] // CHUNK):
            cells = slice(piece * CHUNK, (piece + 1) * CHUNK)
            low = cell_ids[:, cells] & (CHUNK - 1)
            high = lax.shift_right_logical(cell_ids[:, cells], CHUNK.bit_length() - 1)
            picker = (
                (lax.broadcasted_iota(jnp.int32, (CHUNK, CHUNK), 0) == low).astype(jnp.float32).astype(jnp.bfloat16)
            )
            found = jnp.dot(stacked[...], picker, preferred_element_type=jnp.float32)
            result = jnp.zeros((rows, CHUNK), jnp.float32)
            for chunk in range(chunks):
                result = jnp.where(high == chunk, found[chunk * rows : (chunk + 1) * rows], result)
            result_ref[:, cells] = result.astype(jnp.bfloat16)

    select_cells(wanted[depth], chosen.at[depth])
    loads[3].wait()
    loads[4].wait()
    bracket[bracket.shape[0] - TILE :, :] = jnp.zeros((TILE, columns), jnp.int32)
    fraction[fraction.shape[0] - TILE :, :] = jnp.zeros((TILE, columns), jnp.float32)
    bracket[0:levels_out, :] = bracket_in[...]
    fraction[0:levels_out, :] = fraction_in[...]

    for turn, offset in enumerate(offsets):
        slot = offset + depth
        ask(offset).wait_recv()
        select_cells(asked[slot], picked.at[slot])
        answer(offset).start()
        if turn % 2 == 1 and turn // 2 < rounds - 1:
            hear(turn // 2)

    half = slabs // 2
    order = [0] + [p for d in range(1, half) for p in (d, slabs - d)] + [half]
    positions = [
        jnp.minimum(lax.rem(intersection[b] - group + depth + groups, groups), block_count - 1)
        for b in range(block_count)
    ]
    loads[5].wait()
    for offset in offsets:
        answer(offset).wait_recv()
    for turn in range(min(len(offsets) // 2, rounds - 1), rounds):
        hear(turn)
    for target in order:
        block = jnp.zeros((rows, columns), jnp.float32)
        for b in range(block_count):
            block = block + jnp.dot(
                chosen[positions[b]],
                weights[b, :, target * columns : (target + 1) * columns],
                preferred_element_type=jnp.float32,
            )
        outbound[target] = block.astype(jnp.bfloat16)

        @pl.when(target == place)
        def _():
            arrived[target] = outbound[target]

        @pl.when(target != place)
        def _():
            deliver(target).start()

    def blend(origins, start):
        for origin in origins:
            slab[origin] = arrived[origin].astype(jnp.float32)

        def mix(j, carry):
            out_rows = pl.ds(pl.multiple_of(j * TILE, TILE), TILE)
            for piece in range(columns // 128):
                lanes = slice(piece * 128, (piece + 1) * 128)
                share = fraction[out_rows, lanes]
                rest = 1.0 - share
                below = [jnp.zeros((TILE, 128), jnp.float32)] * fields
                above = [jnp.zeros((TILE, 128), jnp.float32)] * fields
                for origin in origins:
                    lower = bracket[out_rows, lanes] - origin * level_slab
                    upper = lower + 1
                    lower_tile, upper_tile = lower >> 3, upper >> 3
                    lower_row, upper_row = lower & (TILE - 1), upper & (TILE - 1)
                    for tile in range(tiles):
                        in_lower, in_upper = lower_tile == tile, upper_tile == tile
                        for field in range(fields):
                            row = field * even + tile * TILE
                            values = slab[origin, row : row + TILE, lanes]
                            below[field] = jnp.where(in_lower, pick_rows(values, lower_row), below[field])
                            above[field] = jnp.where(in_upper, pick_rows(values, upper_row), above[field])
                    for extra in range(odd):
                        at_lower, at_upper = lower == even + extra, upper == even + extra
                        for field in range(fields):
                            row = full_rows + field * odd + extra
                            last = slab[origin, row : row + 1, lanes]
                            below[field] = jnp.where(at_lower, last, below[field])
                            above[field] = jnp.where(at_upper, last, above[field])
                for field in range(fields):
                    mixed = rest * below[field] + share * above[field]
                    if start:
                        total[field, out_rows, lanes] = mixed
                    else:
                        total[field, out_rows, lanes] += mixed
            return carry

        lax.fori_loop(0, total.shape[1] // TILE, mix, 0)

    turns = [order[0:3]] + [order[n : n + 2] for n in range(3, len(order), 2)]
    for n, origins in enumerate(turns):
        for origin in origins:

            @pl.when(origin != place)
            def _():
                await_slab(origin)

        blend(origins, n == 0)

    out_ref[...] = total[:, 0:levels_out, :].astype(jnp.bfloat16)

    for offset in offsets:
        ask(offset).wait_send()
        answer(offset).wait_send()
    for target in order:

        @pl.when(target != place)
        def _():
            deliver(target).wait_send()


def local(groups, slabs, source_state, intersection, index_map, blocks, bracket, fraction):
    fields, level_slab, tile_cells = source_state.shape
    block_count, width = index_map.shape
    levels_out, columns = bracket.shape
    out_rows = -(-levels_out // TILE) * TILE
    chunks = tile_cells // CHUNK
    rows = -(-fields * level_slab // TILE) * TILE
    rounds = slabs // 2 - 1
    any_spec = pl.BlockSpec(memory_space=pl.ANY)
    dma = pltpu.SemaphoreType.DMA

    return pl.pallas_call(
        functools.partial(kernel, groups, slabs),
        out_shape=pltpu.VMEM((fields, levels_out, columns), jnp.bfloat16),
        in_specs=[any_spec] * 6,
        out_specs=pl.BlockSpec(memory_space=pltpu.VMEM),
        scratch_shapes=[
            pltpu.VMEM(source_state.shape, jnp.bfloat16),
            pltpu.SMEM(intersection.shape, jnp.int32),
            pltpu.VMEM(index_map.shape, jnp.int32),
            pltpu.VMEM(blocks.shape, jnp.bfloat16),
            pltpu.VMEM(bracket.shape, jnp.int32),
            pltpu.VMEM(fraction.shape, jnp.float32),
            pltpu.VMEM((out_rows, columns), jnp.int32),
            pltpu.VMEM((out_rows, columns), jnp.float32),
            pltpu.VMEM((rows * chunks, CHUNK), jnp.bfloat16),
            pltpu.VMEM((block_count, 1, width), jnp.int32),
            pltpu.VMEM((block_count, 1, width), jnp.int32),
            pltpu.VMEM((block_count, rows, width), jnp.bfloat16),
            pltpu.VMEM((block_count, rows, width), jnp.bfloat16),
            pltpu.VMEM((slabs, rows, columns), jnp.bfloat16),
            pltpu.VMEM((slabs, rows, columns), jnp.bfloat16),
            pltpu.VMEM((slabs, rows, columns), jnp.float32),
            pltpu.VMEM((fields, out_rows, columns), jnp.float32),
            dma((6,)),
            dma((block_count,)),
            dma((block_count,)),
            dma((block_count,)),
            dma((block_count,)),
            dma((slabs,)),
            dma((slabs,)),
            pltpu.SemaphoreType.REGULAR((rounds,)),
            pltpu.SemaphoreType.REGULAR((rounds,)),
        ],
        compiler_params=pltpu.CompilerParams(
            collective_id=0, has_side_effects=True, vmem_limit_bytes=56 * 1024 * 1024
        ),
        name="regrid",
    )(source_state, intersection, index_map, blocks, bracket, fraction)


def solution(mesh):
    in_specs = (
        P(None, "lev", "horiz"),
        P("horiz"),
        P("horiz", None),
        P("horiz", None, None),
        P(None, ("horiz", "lev")),
        P(None, ("horiz", "lev")),
    )
    out_specs = P(None, None, ("horiz", "lev"))
    body = functools.partial(local, mesh.shape["horiz"], mesh.shape["lev"])
    return jax.shard_map(body, mesh=mesh, in_specs=in_specs, out_specs=out_specs, check_vma=False)
```

time: 33.9 us -> 31.5 us (0.929)
  the two profiles are of different devices: /device:TPU:32 before, /device:TPU:64 now
where the time goes in v4:
time: 31.5 us; the launch traced here: 31.1 us
  Pallas kernels  30.4 us (97%)
  local copies, waits for them, and re-layouts  0.73 us (2%)
    pallas_call x1, Pallas kernels, local(): pl.pallas_call(functools.partial(kernel, groups, slabs), out_shape=pltpu....  30.4 us
    unnamed x1, local copies, waits for them, and re-layouts  0.73 us

profile of v4, /device:TPU:64, one launch (start us, length us, event | category | flops | bytes accessed | tf_op | source)
XLA Modules:
  0.0 31.1 jit_solution(7737757022534226112)
XLA Ops:
  0.0 30.4 %regrid.1 = bf16[5,127,256]{2,1,0:T(8,128)(2,1)S(1)} custom-call(bf16[5,17,4096]{2,1,0:T(8,128)(2,1)} %source_hbm.1, s32[5]{0:T(128)} %intersection_hbm.1, s32[5,512]{1,0:T(8,128)} %index_hbm.1, bf16[5,512,2048]{2,1,0:T(8,128)(2,1)} %blocks_hbm.1, s32[127,256]{1,0:T(8,128)} %bracket_hbm.1, f32[127,256]{1,0:T(8,128)} %fraction_hbm.1), custom_call_target="tpu_custom_call" | custom-call | tf_op jit(solution)/shard_map/regrid/pallas_call | solution.py:308
  30.4 0.7 %copy.8 = bf16[5,127,256]{2,1,0:T(8,128)(2,1)} copy(bf16[5,127,256]{2,1,0:T(8,128)(2,1)S(1)} %regrid.1) | data formatting | bytes 650240

commit v5 on v4

--- a/solution.py
+++ b/solution.py
@@ -66,7 +66,7 @@
     even = tiles * TILE
     full_rows = fields * even
     rows = stacked.shape[0] // chunks
-    offsets = list(range(1, depth + 1)) + list(range(-depth, 0))
+    offsets = list(range(1, depth + 1)) + list(range(-1, -depth - 1, -1))
 
     barrier = pltpu.get_barrier_semaphore()
     for offset in offsets:
@@ -202,8 +202,8 @@
         if turn % 2 == 1 and turn // 2 < rounds - 1:
             hear(turn // 2)
 
-    half = slabs // 2
-    order = [0] + [p for d in range(1, half) for p in (d, slabs - d)] + [half]
+    order = list(range(slabs))
+    awaited = order[: slabs // 2] + order[: slabs // 2 - 1 : -1]
     positions = [
         jnp.minimum(lax.rem(intersection[b] - group + depth + groups, groups), block_count - 1)
         for b in range(block_count)
@@ -272,7 +272,7 @@
 
         lax.fori_loop(0, total.shape[1] // TILE, mix, 0)
 
-    turns = [order[0:3]] + [order[n : n + 2] for n in range(3, len(order), 2)]
+    turns = [awaited[0:3]] + [awaited[n : n + 2] for n in range(3, slabs, 2)]
     for n, origins in enumerate(turns):
         for origin in origins:
 

time: 31.5 us -> 33.8 us (1.073)
  Pallas kernels: 30.4 us -> 33 us
    pallas_call x1, Pallas kernels: 30.4 us -> 33 us  [local(): pl.pallas_call(functools.partial(kernel, groups, slabs), out_shape=pltpu....]
where the time goes in v5:
time: 33.8 us; the launch traced here: 33.7 us
  Pallas kernels  33 us (98%)
  local copies, waits for them, and re-layouts  0.73 us (2%)
    pallas_call x1, Pallas kernels, local(): pl.pallas_call(functools.partial(kernel, groups, slabs), out_shape=pltpu....  33 us
    unnamed x1, local copies, waits for them, and re-layouts  0.73 us

profile of v5, /device:TPU:64, one launch (start us, length us, event | category | flops | bytes accessed | tf_op | source)
XLA Modules:
  0.0 33.7 jit_solution(12656556653892039871)
XLA Ops:
  0.0 33.0 %regrid.1 = bf16[5,127,256]{2,1,0:T(8,128)(2,1)S(1)} custom-call(bf16[5,17,4096]{2,1,0:T(8,128)(2,1)} %source_hbm.1, s32[5]{0:T(128)} %intersection_hbm.1, s32[5,512]{1,0:T(8,128)} %index_hbm.1, bf16[5,512,2048]{2,1,0:T(8,128)(2,1)} %blocks_hbm.1, s32[127,256]{1,0:T(8,128)} %bracket_hbm.1, f32[127,256]{1,0:T(8,128)} %fraction_hbm.1), custom_call_target="tpu_custom_call" | custom-call | tf_op jit(solution)/shard_map/regrid/pallas_call | solution.py:308
  33.0 0.7 %copy.8 = bf16[5,127,256]{2,1,0:T(8,128)(2,1)} copy(bf16[5,127,256]{2,1,0:T(8,128)(2,1)S(1)} %regrid.1) | data formatting | bytes 650240

commit v6 on v5

--- a/solution.py
+++ b/solution.py
@@ -66,7 +66,7 @@
     even = tiles * TILE
     full_rows = fields * even
     rows = stacked.shape[0] // chunks
-    offsets = list(range(1, depth + 1)) + list(range(-1, -depth - 1, -1))
+    offsets = list(range(1, depth + 1)) + list(range(-depth, 0))
 
     barrier = pltpu.get_barrier_semaphore()
     for offset in offsets:
@@ -202,8 +202,10 @@
         if turn % 2 == 1 and turn // 2 < rounds - 1:
             hear(turn // 2)
 
-    order = list(range(slabs))
-    awaited = order[: slabs // 2] + order[: slabs // 2 - 1 : -1]
+    core = lax.rem(group, 2)
+    orders = zip([1, 2, 0, 3, 7, 4, 6, 5], [0, 1, 7, 2, 6, 3, 5, 4])
+    order = [early * core + late * (1 - core) for late, early in orders]
+    awaited = [0, 1, 2, 3, 7, 6, 5, 4]
     positions = [
         jnp.minimum(lax.rem(intersection[b] - group + depth + groups, groups), block_count - 1)
         for b in range(block_count)
@@ -218,7 +220,7 @@
         for b in range(block_count):
             block = block + jnp.dot(
                 chosen[positions[b]],
-                weights[b, :, target * columns : (target + 1) * columns],
+                weights[b, :, pl.ds(pl.multiple_of(target * columns, columns), columns)],
                 preferred_element_type=jnp.float32,
             )
         outbound[target] = block.astype(jnp.bfloat16)
@@ -231,12 +233,14 @@
         def _():
             deliver(target).start()
 
-    def blend(origins, start):
+    def blend(origins, start, finish):
         for origin in origins:
             slab[origin] = arrived[origin].astype(jnp.float32)
 
-        def mix(j, carry):
-            out_rows = pl.ds(pl.multiple_of(j * TILE, TILE), TILE)
+        def mix(j, kept):
+            first = j * TILE if isinstance(j, int) else pl.multiple_of(j * TILE, TILE)
+            out_rows = pl.ds(first, TILE)
+            kept_rows = pl.ds(first, kept)
             for piece in range(columns // 128):
                 lanes = slice(piece * 128, (piece + 1) * 128)
                 share = fraction[out_rows, lanes]
@@ -264,13 +268,21 @@
                             above[field] = jnp.where(at_upper, last, above[field])
                 for field in range(fields):
                     mixed = rest * below[field] + share * above[field]
-                    if start:
+                    if not start:
+                        mixed = total[field, out_rows, lanes] + mixed
+                    if finish:
+                        out_ref[field, kept_rows, lanes] = mixed[0:kept].astype(jnp.bfloat16)
+                    else:
                         total[field, out_rows, lanes] = mixed
-                    else:
-                        total[field, out_rows, lanes] += mixed
+
+        def step(j, carry):
+            mix(j, TILE)
             return carry
 
-        lax.fori_loop(0, total.shape[1] // TILE, mix, 0)
+        whole = levels_out // TILE
+        lax.fori_loop(0, whole, step, 0)
+        if levels_out % TILE:
+            mix(whole, levels_out % TILE)
 
     turns = [awaited[0:3]] + [awaited[n : n + 2] for n in range(3, slabs, 2)]
     for n, origins in enumerate(turns):
@@ -280,14 +292,12 @@
             def _():
                 await_slab(origin)
 
-        blend(origins, n == 0)
-
-    out_ref[...] = total[:, 0:levels_out, :].astype(jnp.bfloat16)
+        blend(origins, n == 0, n == len(turns) - 1)
 
     for offset in offsets:
         ask(offset).wait_send()
         answer(offset).wait_send()
-    for target in order:
+    for target in range(slabs):
 
         @pl.when(target != place)
         def _():

time: 33.8 us -> 29.7 us (0.88)
  Pallas kernels: 33 us -> 28.7 us
    pallas_call x1, Pallas kernels: 33 us -> 28.7 us  [local(): pl.pallas_call(functools.partial(kernel, groups, slabs), out_shape=pltpu....]
where the time goes in v6:
time: 29.7 us; the launch traced here: 29.4 us
  Pallas kernels  28.7 us (97%)
  local copies, waits for them, and re-layouts  0.73 us (2%)
    pallas_call x1, Pallas kernels, local(): pl.pallas_call(functools.partial(kernel, groups, slabs), out_shape=pltpu....  28.7 us
    unnamed x1, local copies, waits for them, and re-layouts  0.73 us

profile of v6, /device:TPU:64, one launch (start us, length us, event | category | flops | bytes accessed | tf_op | source)
XLA Modules:
  0.0 29.4 jit_solution(4084363795489532978)
XLA Ops:
  0.0 28.7 %regrid.1 = bf16[5,127,256]{2,1,0:T(8,128)(2,1)S(1)} custom-call(bf16[5,17,4096]{2,1,0:T(8,128)(2,1)} %source_hbm.1, s32[5]{0:T(128)} %intersection_hbm.1, s32[5,512]{1,0:T(8,128)} %index_hbm.1, bf16[5,512,2048]{2,1,0:T(8,128)(2,1)} %blocks_hbm.1, s32[127,256]{1,0:T(8,128)} %bracket_hbm.1, f32[127,256]{1,0:T(8,128)} %fraction_hbm.1), custom_call_target="tpu_custom_call" | custom-call | tf_op jit(solution)/shard_map/regrid/pallas_call | solution.py:318
  28.7 0.7 %copy.8 = bf16[5,127,256]{2,1,0:T(8,128)(2,1)} copy(bf16[5,127,256]{2,1,0:T(8,128)(2,1)S(1)} %regrid.1) | data formatting | bytes 650240

commit v7 on v6

--- a/solution.py
+++ b/solution.py
@@ -280,7 +280,7 @@
             return carry
 
         whole = levels_out // TILE
-        lax.fori_loop(0, whole, step, 0)
+        lax.fori_loop(0, whole, step, 0, unroll=3)
         if levels_out % TILE:
             mix(whole, levels_out % TILE)
 

time: 29.7 us -> 29.5 us (level)
  Pallas kernels: 28.7 us -> 28.4 us
where the time goes in v7:
time: 29.5 us; the launch traced here: 29.2 us
  Pallas kernels  28.4 us (96%)
  local copies, waits for them, and re-layouts  0.73 us (2%)
    pallas_call x1, Pallas kernels, local(): pl.pallas_call(functools.partial(kernel, groups, slabs), out_shape=pltpu....  28.4 us
    unnamed x1, local copies, waits for them, and re-layouts  0.73 us

profile of v7, /device:TPU:64, one launch (start us, length us, event | category | flops | bytes accessed | tf_op | source)
XLA Modules:
  0.0 29.2 jit_solution(6536386750835572909)
XLA Ops:
  0.0 28.4 %regrid.1 = bf16[5,127,256]{2,1,0:T(8,128)(2,1)S(1)} custom-call(bf16[5,17,4096]{2,1,0:T(8,128)(2,1)} %source_hbm.1, s32[5]{0:T(128)} %intersection_hbm.1, s32[5,512]{1,0:T(8,128)} %index_hbm.1, bf16[5,512,2048]{2,1,0:T(8,128)(2,1)} %blocks_hbm.1, s32[127,256]{1,0:T(8,128)} %bracket_hbm.1, f32[127,256]{1,0:T(8,128)} %fraction_hbm.1), custom_call_target="tpu_custom_call" | custom-call | tf_op jit(solution)/shard_map/regrid/pallas_call | solution.py:318
  28.5 0.7 %copy.8 = bf16[5,127,256]{2,1,0:T(8,128)(2,1)} copy(bf16[5,127,256]{2,1,0:T(8,128)(2,1)S(1)} %regrid.1) | data formatting | bytes 650240

commit v8 on v7

--- a/solution.py
+++ b/solution.py
@@ -43,6 +43,7 @@
     arrived,
     slab,
     total,
+    partial,
     local_sem,
     ask_send,
     ask_recv,
@@ -206,23 +207,32 @@
     orders = zip([1, 2, 0, 3, 7, 4, 6, 5], [0, 1, 7, 2, 6, 3, 5, 4])
     order = [early * core + late * (1 - core) for late, early in orders]
     awaited = [0, 1, 2, 3, 7, 6, 5, 4]
-    positions = [
-        jnp.minimum(lax.rem(intersection[b] - group + depth + groups, groups), block_count - 1)
-        for b in range(block_count)
-    ]
+    def block_of(offset):
+        target = lax.rem(group + offset + groups, groups)
+        number = jnp.int32(0)
+        for b in range(block_count):
+            number = number + jnp.where(intersection[b] == target, b, 0)
+        return jnp.minimum(number, block_count - 1)
+
+    def product(target, offset):
+        return jnp.dot(
+            chosen[offset + depth],
+            weights[block_of(offset), :, pl.ds(pl.multiple_of(target * columns, columns), columns)],
+            preferred_element_type=jnp.float32,
+        )
+
     loads[5].wait()
-    for offset in offsets:
+    ready = offsets[:depth]
+    for offset in ready:
+        answer(offset).wait_recv()
+    for target in order:
+        partial[target] = sum([product(target, offset) for offset in ready], product(target, 0))
+    for offset in offsets[depth:]:
         answer(offset).wait_recv()
     for turn in range(min(len(offsets) // 2, rounds - 1), rounds):
         hear(turn)
     for target in order:
-        block = jnp.zeros((rows, columns), jnp.float32)
-        for b in range(block_count):
-            block = block + jnp.dot(
-                chosen[positions[b]],
-                weights[b, :, pl.ds(pl.multiple_of(target * columns, columns), columns)],
-                preferred_element_type=jnp.float32,
-            )
+        block = sum([product(target, offset) for offset in offsets[depth:]], partial[target])
         outbound[target] = block.astype(jnp.bfloat16)
 
         @pl.when(target == place)
@@ -338,6 +348,7 @@
             pltpu.VMEM((slabs, rows, columns), jnp.bfloat16),
             pltpu.VMEM((slabs, rows, columns), jnp.float32),
             pltpu.VMEM((fields, out_rows, columns), jnp.float32),
+            pltpu.VMEM((slabs, rows, columns), jnp.float32),
             dma((6,)),
             dma((block_count,)),
             dma((block_count,)),

time: 29.5 us -> 29 us (0.983)
  Pallas kernels: 28.4 us -> 27.8 us
    pallas_call x1, Pallas kernels: 28.4 us -> 27.8 us  [local(): pl.pallas_call(functools.partial(kernel, groups, slabs), out_shape=pltpu....]
where the time goes in v8:
time: 29 us; the launch traced here: 28.5 us
  Pallas kernels  27.8 us (96%)
  local copies, waits for them, and re-layouts  0.73 us (3%)
    pallas_call x1, Pallas kernels, local(): pl.pallas_call(functools.partial(kernel, groups, slabs), out_shape=pltpu....  27.8 us
    unnamed x1, local copies, waits for them, and re-layouts  0.73 us

profile of v8, /device:TPU:64, one launch (start us, length us, event | category | flops | bytes accessed | tf_op | source)
XLA Modules:
  0.0 28.5 jit_solution(12217541111051333787)
XLA Ops:
  0.0 27.8 %regrid.1 = bf16[5,127,256]{2,1,0:T(8,128)(2,1)S(1)} custom-call(bf16[5,17,4096]{2,1,0:T(8,128)(2,1)} %source_hbm.1, s32[5]{0:T(128)} %intersection_hbm.1, s32[5,512]{1,0:T(8,128)} %index_hbm.1, bf16[5,512,2048]{2,1,0:T(8,128)(2,1)} %blocks_hbm.1, s32[127,256]{1,0:T(8,128)} %bracket_hbm.1, f32[127,256]{1,0:T(8,128)} %fraction_hbm.1), custom_call_target="tpu_custom_call" | custom-call | tf_op jit(solution)/shard_map/regrid/pallas_call | solution.py:328
  27.8 0.7 %copy.8 = bf16[5,127,256]{2,1,0:T(8,128)(2,1)} copy(bf16[5,127,256]{2,1,0:T(8,128)(2,1)S(1)} %regrid.1) | data formatting | bytes 650240

commit v9 on v8

--- a/solution.py
+++ b/solution.py
@@ -227,12 +227,15 @@
         answer(offset).wait_recv()
     for target in order:
         partial[target] = sum([product(target, offset) for offset in ready], product(target, 0))
-    for offset in offsets[depth:]:
-        answer(offset).wait_recv()
+    nearer, farther = core - 2, -1 - core
+    answer(nearer).wait_recv()
+    for target in order:
+        partial[target] += product(target, nearer)
+    answer(farther).wait_recv()
     for turn in range(min(len(offsets) // 2, rounds - 1), rounds):
         hear(turn)
     for target in order:
-        block = sum([product(target, offset) for offset in offsets[depth:]], partial[target])
+        block = partial[target] + product(target, farther)
         outbound[target] = block.astype(jnp.bfloat16)
 
         @pl.when(target == place)

time: 29 us -> 29.9 us (1.031); the launches traced: 28.5 us -> 29.9 us
  Pallas kernels: 27.8 us -> 29.1 us
    pallas_call x1, Pallas kernels: 27.8 us -> 29.1 us  [local(): pl.pallas_call(functools.partial(kernel, groups, slabs), out_shape=pltpu....]
where the time goes in v9:
time: 29.9 us
  Pallas kernels  29.1 us (97%)
  local copies, waits for them, and re-layouts  0.73 us (2%)
    pallas_call x1, Pallas kernels, local(): pl.pallas_call(functools.partial(kernel, groups, slabs), out_shape=pltpu....  29.1 us
    unnamed x1, local copies, waits for them, and re-layouts  0.73 us

profile of v9, /device:TPU:64, one launch (start us, length us, event | category | flops | bytes accessed | tf_op | source)
XLA Modules:
  0.0 29.9 jit_solution(3798333695152779120)
XLA Ops:
  0.0 29.1 %regrid.1 = bf16[5,127,256]{2,1,0:T(8,128)(2,1)S(1)} custom-call(bf16[5,17,4096]{2,1,0:T(8,128)(2,1)} %source_hbm.1, s32[5]{0:T(128)} %intersection_hbm.1, s32[5,512]{1,0:T(8,128)} %index_hbm.1, bf16[5,512,2048]{2,1,0:T(8,128)(2,1)} %blocks_hbm.1, s32[127,256]{1,0:T(8,128)} %bracket_hbm.1, f32[127,256]{1,0:T(8,128)} %fraction_hbm.1), custom_call_target="tpu_custom_call" | custom-call | tf_op jit(solution)/shard_map/regrid/pallas_call | solution.py:331
  29.1 0.7 %copy.8 = bf16[5,127,256]{2,1,0:T(8,128)(2,1)} copy(bf16[5,127,256]{2,1,0:T(8,128)(2,1)S(1)} %regrid.1) | data formatting | bytes 650240
